TPU v7x, 32 devices: a whole 2x2x4 slice. The times are simulated.
32 devices in a mesh: stream: 4 (over x, core), cross: 8 (over z, y).
Axes of the slice: x: 2, y: 2, z: 4, core: 2. Of those that a mesh axis runs over, the one named last changes fastest.
Arguments:
- state_now: float32 [7, 8, 64, 512], P(None, None, 'cross', 'stream'), as said below
- state_base: float32 [7, 8, 64, 512], P(None, None, 'cross', 'stream'), as said below
- inflow: float32 [7, 8, 64, 3], P(None, None, 'cross'), as said below
Outputs:
- state_next: float32 [7, 8, 64, 512], P(None, None, 'cross', 'stream')
Inputs may be any that keep to these rules, and one draw needn't show every extreme that they name: `state_now`: partial densities and volume fractions are positive, volume fractions below 1, and the pressure that each cell implies is positive. `state_base`: partial densities and volume fractions are positive, volume fractions below 1, and the pressure that each cell implies is positive. `inflow`: partial densities and volume fractions are positive, volume fractions below 1, and the pressure that each cell implies is positive.
All inputs are finite; a program needn't handle non-finite values.
Results may differ from a plain program's by a relative error of at most 0.0003.
Values sent between devices are 32-bit elements; how exact they have to be, the bound alone decides.
A program may use at most 64 MiB of HBM per device.

v0:
```python
import functools

import jax
import jax.numpy as jnp
from jax import lax
from jax.experimental import pallas as pl
from jax.experimental.pallas import tpu as pltpu
from jax.sharding import PartitionSpec as P

MESH = pl.DeviceIdType.MESH
VARS = 7
HALO = 3
GROUP = 8
STIFF = 4.4 * 0.6 / 3.4


def recip(x):
    return 1.0 / x


def mixture(volume):
    rest = 1.0 - volume
    return volume * (1.0 / 0.4) + rest * (1.0 / 3.4), rest * STIFF


def primitive(u):
    inv = recip(u[0] + u[1])
    vx, vy, vz = u[2] * inv, u[3] * inv, u[4] * inv
    gam, stiff = mixture(u[6])
    kinetic = 0.5 * (u[2] * vx + u[3] * vy + u[4] * vz)
    return [u[0], u[1], vx, vy, vz, (u[5] - kinetic - stiff) * recip(gam), u[6]]


def max_speed(w):
    gam, stiff = mixture(w[6])
    top = (gam + 1.0) * w[5] + stiff
    sound = jnp.sqrt(top * recip(gam * (w[0] + w[1])))
    return jnp.maximum(jnp.maximum(jnp.abs(w[2]), jnp.abs(w[3])), jnp.abs(w[4])) + sound


def weno_pair(f, g, h, k, l):
    e1, e2, e3, e4 = g - f, h - g, k - h, l - k
    s0, s1, s2 = e2 - e1, e3 - e2, e4 - e3
    d2, d3 = e2 + e2, e3 + e3
    t0, t1, t2 = d2 + s0, e2 + e3, d3 - s2
    eps = 1e-6 * 12.0 / 13.0
    r0 = recip(s0 * s0 + (eps + (3.0 / 13.0) * (t0 * t0)))
    r1 = recip(s1 * s1 + (eps + (3.0 / 13.0) * (t1 * t1)))
    r2 = recip(s2 * s2 + (eps + (3.0 / 13.0) * (t2 * t2)))
    a0, a1, a2 = r0 * r0, 6.0 * (r1 * r1), r2 * r2
    b0, b2 = 3.0 * a0, 3.0 * a2
    p0, p2 = t0 + e2, t2 + e3
    up = (a0 * (p0 + s0) + a1 * (d3 + e2) + b2 * p2) * recip(6.0 * (a0 + a1 + b2))
    down = (a2 * (p2 - s2) + a1 * (d2 + e3) + b0 * p0) * recip(6.0 * (a2 + a1 + b0))
    return h + up, h - down


def limit(state, low, high):
    out = list(state)
    for v in (0, 1, 5):
        out[v] = jnp.maximum(state[v], low[v])
    out[6] = jnp.minimum(jnp.maximum(state[6], low[6]), high)
    return out


def side(w, normal):
    dens = w[0] + w[1]
    gam, stiff = mixture(w[6])
    m = [dens * w[2], dens * w[3], dens * w[4]]
    heat = gam * w[5] + stiff
    energy = heat + 0.5 * (m[0] * w[2] + m[1] * w[3] + m[2] * w[4])
    vn = w[2 + normal]
    amounts = [w[0], w[1], m[0], m[1], m[2], energy, w[6]]
    moved = [q * vn for q in amounts]
    moved[2 + normal] = moved[2 + normal] + w[5]
    moved[5] = (energy + w[5]) * vn
    sound = jnp.sqrt((heat + w[5]) * recip(gam * dens))
    return amounts, moved, vn, jnp.abs(vn) + sound


def faces(left, right, below, above, normal):
    low = {v: 0.5 * jnp.minimum(below[v], above[v]) for v in (0, 1, 5, 6)}
    high = 1.0 - 0.5 * (1.0 - jnp.maximum(below[6], above[6]))
    ul, fl, nl, sl = side(limit(left, low, high), normal)
    ur, fr, nr, sr = side(limit(right, low, high), normal)
    fast = 0.5 * jnp.maximum(sl, sr)
    out = [0.5 * (fl[v] + fr[v]) - fast * (ur[v] - ul[v]) for v in range(VARS)]
    return out + [0.5 * (nl + nr)]


def rate(lo, hi, volume):
    out = [lo[v] - hi[v] for v in range(VARS)]
    out[6] = out[6] + volume * (hi[7] - lo[7])
    return out


def sweep(src, first, count, height, normal, emit):
    base = HALO + first

    def at(c, v):
        return src[pl.ds(pl.multiple_of((c * VARS + v) * height, height), height), :]

    def states(c):
        return [weno_pair(*[at(c + o, v) for o in range(-2, 3)]) for v in range(VARS)]

    def cell(c, left):
        pairs = states(c)
        flux = faces(
            left,
            [p[1] for p in pairs],
            [at(c - 1, v) for v in range(VARS)],
            [at(c, v) for v in range(VARS)],
            normal,
        )
        return flux, [p[0] for p in pairs]

    left = [p[0] for p in states(base - 1)]
    flux, left = cell(base, left)

    def step(i, carry):
        left, lo = carry
        hi, left = cell(i + base + 1, left)
        out = rate(lo, hi, at(i + base, 6))
        emit(i + first, out)
        return left, hi

    lax.fori_loop(0, count, step, (left, flux))


def kernel(
    dims,
    now_hbm,
    base_hbm,
    inflow_hbm,
    kept,
    total,
    scale,
    now,
    base,
    inflow,
    flat,
    wide,
    wz,
    wy,
    shifted,
    sided,
    fluxes,
    pack,
    from_low,
    from_high,
    top_cross,
    top_stream,
    mine,
    load_sem,
    halo_send,
    halo_recv,
    cross_send,
    cross_recv,
    stream_send,
    stream_recv,
):
    n_stream, n_cross, cz, ny, nx = dims
    tile = VARS * ny
    ztile = VARS * cz
    half = cz * GROUP
    ms, mc = lax.axis_index("stream"), lax.axis_index("cross")

    barrier = pltpu.get_barrier_semaphore()
    for d in range(1, n_cross):
        pl.semaphore_signal(
            barrier, device_id={"cross": lax.rem(mc + d, n_cross)}, device_id_type=MESH
        )
    for d in range(1, n_stream):
        pl.semaphore_signal(
            barrier, device_id={"stream": lax.rem(ms + d, n_stream)}, device_id_type=MESH
        )
    loads = [
        pltpu.make_async_copy(now_hbm, now, load_sem.at[0]),
        pltpu.make_async_copy(base_hbm, base, load_sem.at[1]),
        pltpu.make_async_copy(inflow_hbm, inflow, load_sem.at[2]),
    ]
    for copy in loads:
        copy.start()
    loads[0].wait()

    lane = lax.broadcasted_iota(jnp.int32, (ny, nx), 1)
    group = lane // GROUP
    packed = [None] * VARS
    for z in range(cz):
        w = primitive([now[v, z] for v in range(VARS)])
        spots = [HALO + z]
        if z < HALO:
            spots.append(HALO + cz + z)
        if z >= cz - HALO:
            spots.append(z - (cz - HALO))
        for v in range(VARS):
            for c in spots:
                wz[pl.ds(c * tile + v * ny, ny), :] = w[v]
            upper = pltpu.roll(w[v], (GROUP * z - (nx - 5)) % nx, 1)
            lower = pltpu.roll(w[v], (half + GROUP * z + HALO) % nx, 1)
            piece = jnp.where(group == z, upper, lower)
            if z == 0:
                packed[v] = piece
            else:
                packed[v] = jnp.where((group == z) | (group == cz + z), piece, packed[v])
    for v in range(VARS):
        pack[pl.ds(v * ny, ny), :] = packed[v]
    for y in range(ny):
        for v in range(VARS):
            wy[pl.ds((HALO + y) * ztile + v * cz, cz), :] = wz[
                pl.ds(HALO * tile + v * ny + y, cz, stride=tile), :
            ]
    loads[1].wait()
    speed = None
    for z in range(cz):
        s = max_speed(primitive([base[v, z] for v in range(VARS)]))
        speed = s if speed is None else jnp.maximum(speed, s)
    mine[0] = jnp.max(speed, axis=0, keepdims=True)

    pl.semaphore_wait(barrier, n_cross - 1 + n_stream - 1)

    rows = HALO * ztile
    halo_y = [
        pltpu.make_async_remote_copy(
            src_ref=wy.at[pl.ds(rows, rows)],
            dst_ref=wy.at[pl.ds((HALO + ny) * ztile, rows)],
            send_sem=halo_send.at[0],
            recv_sem=halo_recv.at[0],
            device_id={"cross": lax.rem(mc + n_cross - 1, n_cross)},
            device_id_type=MESH,
        ),
        pltpu.make_async_remote_copy(
            src_ref=wy.at[pl.ds(ny * ztile, rows)],
            dst_ref=wy.at[pl.ds(0, rows)],
            send_sem=halo_send.at[1],
            recv_sem=halo_recv.at[1],
            device_id={"cross": lax.rem(mc + 1, n_cross)},
            device_id_type=MESH,
        ),
    ]
    to_high = pltpu.make_async_remote_copy(
        src_ref=pack,
        dst_ref=from_low,
        send_sem=halo_send.at[2],
        recv_sem=halo_recv.at[2],
        device_id={"stream": lax.rem(ms + 1, n_stream)},
        device_id_type=MESH,
    )
    to_low = pltpu.make_async_remote_copy(
        src_ref=pack,
        dst_ref=from_high,
        send_sem=halo_send.at[3],
        recv_sem=halo_recv.at[3],
        device_id={"stream": lax.rem(ms + n_stream - 1, n_stream)},
        device_id_type=MESH,
    )

    def reduce_copies(slot, buffer, axis, size, me, send, recv):
        return [
            pltpu.make_async_remote_copy(
                src_ref=mine.at[slot],
                dst_ref=buffer.at[d - 1],
                send_sem=send.at[d - 1],
                recv_sem=recv.at[d - 1],
                device_id={axis: lax.rem(me + d, size)},
                device_id_type=MESH,
            )
            for d in range(1, size)
        ]

    over_cross = reduce_copies(0, top_cross, "cross", n_cross, mc, cross_send, cross_recv)
    over_stream = reduce_copies(1, top_stream, "stream", n_stream, ms, stream_send, stream_recv)

    for copy in over_cross:
        copy.start()

    @pl.when(ms < n_stream - 1)
    def _():
        to_high.start()

    @pl.when(ms > 0)
    def _():
        to_low.start()

    for copy in halo_y:
        copy.start()
    loads[2].wait()

    def stream_shifts(w):
        return [[pltpu.roll(x, d % nx, 1) for x in w] for d in (2, 1, -1, -2)]

    def stream_states(shifts, w):
        m2, m1, p1, p2 = shifts
        pairs = [weno_pair(m2[v], m1[v], w[v], p1[v], p2[v]) for v in range(VARS)]
        return [pltpu.roll(p[0], 1, 1) for p in pairs], [p[1] for p in pairs]

    def ahead(lo):
        return [pltpu.roll(f, nx - 1, 1) for f in lo]

    def cell_rows(v, z):
        return pl.ds(pl.multiple_of((v * cz + z) * ny, ny), ny)

    def keep_rate(z, out):
        for v in range(VARS):
            total[cell_rows(v, z), :] = out[v]

    sweep(wz, 0, cz, ny, 2, keep_rate)

    whole = (lane >= HALO) & (lane < nx - 2)

    def centre(z):
        return [
            wz[pl.ds(pl.multiple_of(((HALO + z) * VARS + v) * ny, ny), ny), :]
            for v in range(VARS)
        ]

    def stage_shift(z):
        for d, row in enumerate(stream_shifts(centre(z))):
            for v in range(VARS):
                shifted[d, v] = row[v]

    def stage_state(z):
        shifts = [[shifted[d, v] for v in range(VARS)] for d in range(4)]
        left, right = stream_states(shifts, centre(z))
        for v in range(VARS):
            sided[0, v] = left[v]
            sided[1, v] = right[v]
            sided[2, v] = shifts[1][v]

    def stage_flux(z):
        left, right, below = [[sided[k, v] for v in range(VARS)] for k in range(3)]
        lo = [jnp.where(whole, f, 0.0) for f in faces(left, right, below, centre(z), 0)]
        hi = ahead(lo)
        for o in range(VARS + 1):
            fluxes[0, o] = lo[o]
            fluxes[1, o] = hi[o]

    def stage_rate(z):
        lo, hi = [[fluxes[k, o] for o in range(VARS + 1)] for k in range(2)]
        out = rate(lo, hi, centre(z)[6])
        for v in range(VARS):
            total[cell_rows(v, z), :] = total[cell_rows(v, z), :] + out[v]

    stages = (stage_shift, stage_state, stage_flux, stage_rate)
    depth = len(stages)

    def advance(z):
        for k in reversed(range(depth)):
            stages[k](z - k)

    for z in range(depth - 1):
        for k in reversed(range(z + 1)):
            stages[k](z - k)
    lax.fori_loop(depth - 1, cz, lambda z, c: (advance(z), c)[1], 0)
    for z in range(cz, cz + depth - 1):
        for k in reversed(range(z - cz + 1, depth)):
            stages[k](z - k)

    for copy in over_cross:
        copy.wait_recv()
    slab = mine[0]
    for d in range(1, n_cross):
        slab = jnp.maximum(slab, top_cross[d - 1])
    mine[1] = slab

    @pl.when(ms == 0)
    def _():
        for k in range(HALO):
            for v in range(VARS):
                flat[k, :, pl.ds(v * ny, ny)] = inflow[v, k]
            wide[pl.ds(half + k, cz, stride=GROUP), :] = flat[k]
        turned = jnp.transpose(wide[...])
        w = primitive([turned[v * ny : (v + 1) * ny] for v in range(VARS)])
        for v in range(VARS):
            from_low[pl.ds(v * ny, ny), :] = w[v]

    for copy in over_stream:
        copy.start()

    @pl.when(ms > 0)
    def _():
        to_high.wait_recv()

    spot = lane % GROUP

    @pl.when(ms == n_stream - 1)
    def _():
        for v in range(VARS):
            own = pack[pl.ds(v * ny, ny), :]
            copies = [pltpu.roll(own, k, 1) for k in (1, 2, 3)]
            from_high[pl.ds(v * ny, ny), :] = jnp.where(
                spot == 5, copies[0], jnp.where(spot == 6, copies[1], copies[2])
            )

    @pl.when(ms < n_stream - 1)
    def _():
        to_low.wait_recv()

    upper_side = lane < half
    edge = []
    for v in range(VARS):
        own = pack[pl.ds(v * ny, ny), :]
        low, high = from_low[pl.ds(v * ny, ny), :], from_high[pl.ds(v * ny, ny), :]
        edge.append(
            jnp.where(
                upper_side,
                jnp.where(spot < 5, own, high),
                jnp.where(spot < HALO, low, own),
            )
        )
    shifts = stream_shifts(edge)
    edge_left, edge_right = stream_states(shifts, edge)
    edge_faces = faces(edge_left, edge_right, shifts[1], edge, 0)
    middle = (spot >= HALO) & (spot < 2 * HALO)
    lo = [jnp.where(middle, f, 0.0) for f in edge_faces]
    hi = ahead(lo)
    merged = []
    for out in rate(lo, hi, edge[6]):
        upper = jnp.where(upper_side & (spot >= 2) & (spot < 5), out, 0.0)
        lower = jnp.where(jnp.logical_not(upper_side) & middle, out, 0.0)
        merged.append(upper + pltpu.roll(lower, nx - half + 2, 1))
    rim = (lane < HALO) | (lane >= nx - HALO)
    for z in range(cz):
        for v in range(VARS):
            patch = pltpu.roll(merged[v], (nx - HALO - 2 - GROUP * z) % nx, 1)
            rows = cell_rows(v, z)
            total[rows, :] = total[rows, :] + jnp.where(rim, patch, 0.0)
            kept[rows, :] = base[v, z] * (1.0 / 3.0) + (2.0 / 3.0) * now[v, z]

    def add_rate(y, out):
        for v in range(VARS):
            rows = pl.ds(v * cz * ny + y, cz, stride=ny)
            total[rows, :] = total[rows, :] + out[v]

    sweep(wy, HALO, ny - 2 * HALO, cz, 1, add_rate)
    halo_y[0].wait_recv()
    sweep(wy, ny - HALO, HALO, cz, 1, add_rate)
    halo_y[1].wait_recv()
    sweep(wy, 0, HALO, cz, 1, add_rate)

    for copy in over_stream:
        copy.wait_recv()
    top = mine[1]
    for d in range(1, n_stream):
        top = jnp.maximum(top, top_stream[d - 1])
    step = (2.0 / 3.0 * 0.3) / jnp.max(top, keepdims=True)
    scale[...] = jnp.broadcast_to(step, (ny, nx))

    for copy in halo_y + over_cross + over_stream:
        copy.wait_send()

    @pl.when(ms < n_stream - 1)
    def _():
        to_high.wait_send()

    @pl.when(ms > 0)
    def _():
        to_low.wait_send()


def finish(ny, kept, total, scale, out_ref):
    step = scale[...]
    for i in range(kept.shape[0] // ny):
        rows = pl.ds(i * ny, ny)
        out_ref[rows, :] = kept[rows, :] + step * total[rows, :]


def solution(mesh):
    n_stream, n_cross = mesh.shape["stream"], mesh.shape["cross"]

    def shards(state_now, state_base, inflow):
        _, cz, ny, nx = state_now.shape
        f32 = jnp.float32
        vmem = lambda *shape: pltpu.VMEM(shape, f32)
        dma = lambda n: pltpu.SemaphoreType.DMA((n,))
        cells = VARS * cz * ny
        kept, total, scale = pl.pallas_call(
            functools.partial(kernel, (n_stream, n_cross, cz, ny, nx)),
            out_shape=(
                vmem(cells, nx),
                vmem(cells, nx),
                vmem(ny, nx),
            ),
            in_specs=[pl.BlockSpec(memory_space=pl.ANY)] * 3,
            out_specs=[pl.BlockSpec(memory_space=pltpu.VMEM)] * 3,
            scratch_shapes=[
                vmem(*state_now.shape),
                vmem(*state_now.shape),
                vmem(VARS, HALO, cz, ny),
                vmem(HALO, cz, nx),
                vmem(nx, nx),
                vmem((cz + 2 * HALO) * VARS * ny, nx),
                vmem((ny + 2 * HALO) * VARS * cz, nx),
                vmem(4, VARS, ny, nx),
                vmem(3, VARS, ny, nx),
                vmem(2, VARS + 1, ny, nx),
                vmem(VARS * ny, nx),
                vmem(VARS * ny, nx),
                vmem(VARS * ny, nx),
                vmem(n_cross - 1, 1, nx),
                vmem(n_stream - 1, 1, nx),
                vmem(2, 1, nx),
                dma(3),
                dma(4),
                dma(4),
                dma(n_cross - 1),
                dma(n_cross - 1),
                dma(n_stream - 1),
                dma(n_stream - 1),
            ],
            compiler_params=pltpu.CompilerParams(collective_id=0, has_side_effects=True),
        )(state_now, state_base, jnp.transpose(inflow, (0, 3, 1, 2)))
        kept, total, scale = [
            pltpu.with_memory_space_constraint(x, pltpu.VMEM) for x in (kept, total, scale)
        ]
        out = pl.pallas_call(
            functools.partial(finish, ny),
            out_shape=jax.ShapeDtypeStruct((cells, nx), f32),
            in_specs=[pl.BlockSpec(memory_space=pltpu.VMEM)] * 3,
            out_specs=pl.BlockSpec(memory_space=pltpu.VMEM),
        )(kept, total, scale)
        return out.reshape(state_now.shape)

    split = P(None, None, "cross", "stream")
    return jax.shard_map(
        shards,
        mesh=mesh,
        in_specs=(split, split, P(None, None, "cross", None)),
        out_specs=split,
        check_vma=False,
    )
```

profile of v0, /device:TPU:0, one launch (start us, length us, event | category | flops | bytes accessed | tf_op | source)
XLA Modules:
  0.0 13.1 jit_solution(1815638883781276713)
XLA Ops:
  0.0 12.4 %shard_map.37 = (f32[448,128]{1,0:T(8,128)S(1)}, f32[448,128]{1,0:T(8,128)S(1)}, f32[8,128]{1,0:T(8,128)S(1)}) custom-call(f32[7,8,8,128]{3,2,1,0:T(8,128)} %now_hbm.1, f32[7,8,8,128]{3,2,1,0:T(8,128)} %base_hbm.1, f32[7,3,8,8]{3,2,1,0:T(8,128)} %bitcast.2), custom_call_target="tpu_custom_call" | custom-call | tf_op jit(solution)/shard_map/pallas_call | solution.py:477
  12.4 0.7 %shard_map.38 = f32[448,128]{1,0:T(8,128)} custom-call(f32[448,128]{1,0:T(8,128)S(1)} %get-tuple-element.8.kept, f32[448,128]{1,0:T(8,128)S(1)} %get-tuple-element.9.total, f32[8,128]{1,0:T(8,128)S(1)} %get-tuple-element.10.scale), custom_call_target="tpu_custom_call" | custom-call | tf_op jit(solution)/shard_map/pallas_call | solution.py:516
where the time goes:
time: 13.2 us; the launch traced here: 13.1 us
  Pallas kernels  13.1 us (99%)
    pallas_call x1, Pallas kernels, shards(): pl.pallas_call(functools.partial(kernel, (n_stream, n_cross, cz, ny, nx))...  12.4 us
    pallas_call x1, Pallas kernels, shards(): pl.pallas_call(functools.partial(finish, ny), out_shape=jax.ShapeDtypeStr...  0.71 us

commit v1 on v0

--- a/solution.py
+++ b/solution.py
@@ -11,6 +11,8 @@
 VARS = 7
 HALO = 3
 GROUP = 8
+DIRECT = 64
+HUBS = 2
 STIFF = 4.4 * 0.6 / 3.4
 
 
@@ -94,34 +96,33 @@
     return out
 
 
-def sweep(src, first, count, height, normal, emit):
-    base = HALO + first
-
+def reader(src, height):
     def at(c, v):
         return src[pl.ds(pl.multiple_of((c * VARS + v) * height, height), height), :]
 
+    def row(c):
+        return [at(c, v) for v in range(VARS)]
+
     def states(c):
-        return [weno_pair(*[at(c + o, v) for o in range(-2, 3)]) for v in range(VARS)]
+        pairs = [weno_pair(*[at(c + o, v) for o in range(-2, 3)]) for v in range(VARS)]
+        return [p[0] for p in pairs], [p[1] for p in pairs]
+
+    return at, row, states
+
+
+def sweep(src, count, height, normal, emit):
+    at, row, states = reader(src, height)
 
     def cell(c, left):
-        pairs = states(c)
-        flux = faces(
-            left,
-            [p[1] for p in pairs],
-            [at(c - 1, v) for v in range(VARS)],
-            [at(c, v) for v in range(VARS)],
-            normal,
-        )
-        return flux, [p[0] for p in pairs]
-
-    left = [p[0] for p in states(base - 1)]
-    flux, left = cell(base, left)
+        after, right = states(c)
+        return faces(left, right, row(c - 1), row(c), normal), after
+
+    flux, left = cell(HALO, states(HALO - 1)[0])
 
     def step(i, carry):
         left, lo = carry
-        hi, left = cell(i + base + 1, left)
-        out = rate(lo, hi, at(i + base, 6))
-        emit(i + first, out)
+        hi, left = cell(i + HALO + 1, left)
+        emit(i, rate(lo, hi, at(i + HALO, 6)))
         return left, hi
 
     lax.fori_loop(0, count, step, (left, flux))
@@ -129,6 +130,7 @@
 
 def kernel(
     dims,
+    direct,
     now_hbm,
     base_hbm,
     inflow_hbm,
@@ -148,16 +150,17 @@
     pack,
     from_low,
     from_high,
-    top_cross,
-    top_stream,
+    joint,
+    top_first,
+    top_second,
     mine,
     load_sem,
     halo_send,
     halo_recv,
-    cross_send,
-    cross_recv,
-    stream_send,
-    stream_recv,
+    first_send,
+    first_recv,
+    second_send,
+    second_recv,
 ):
     n_stream, n_cross, cz, ny, nx = dims
     tile = VARS * ny
@@ -165,24 +168,126 @@
     half = cz * GROUP
     ms, mc = lax.axis_index("stream"), lax.axis_index("cross")
 
-    barrier = pltpu.get_barrier_semaphore()
-    for d in range(1, n_cross):
-        pl.semaphore_signal(
-            barrier, device_id={"cross": lax.rem(mc + d, n_cross)}, device_id_type=MESH
-        )
-    for d in range(1, n_stream):
-        pl.semaphore_signal(
-            barrier, device_id={"stream": lax.rem(ms + d, n_stream)}, device_id_type=MESH
-        )
     loads = [
-        pltpu.make_async_copy(now_hbm, now, load_sem.at[0]),
-        pltpu.make_async_copy(base_hbm, base, load_sem.at[1]),
+        pltpu.make_async_copy(base_hbm, base, load_sem.at[0]),
+        pltpu.make_async_copy(now_hbm, now, load_sem.at[1]),
         pltpu.make_async_copy(inflow_hbm, inflow, load_sem.at[2]),
     ]
     for copy in loads:
         copy.start()
+
+    size = n_stream * n_cross
+    across = [(0, d) for d in range(1, n_cross)]
+    along = [(d, 0) for d in range(1, n_stream)]
+    others = [(d, e) for e in range(n_cross) for d in range(n_stream) if (d, e) != (0, 0)]
+    inner, outer = ms > 0, ms < n_stream - 1
+    hubs = [(ms == h) & (mc == 0) for h in range(HUBS)]
+    early = functools.reduce(jnp.logical_or, hubs)
+    caster = hubs[HUBS - 1]
+
+    def device(offset):
+        return {
+            "stream": lax.rem(ms + offset[0], n_stream),
+            "cross": lax.rem(mc + offset[1], n_cross),
+        }
+
+    barrier = pltpu.get_barrier_semaphore()
+
+    def greet(target):
+        pl.semaphore_signal(barrier, device_id=target, device_id_type=MESH)
+
+    if direct:
+        for h in range(HUBS):
+
+            @pl.when(jnp.logical_not(hubs[h]))
+            def _(h=h):
+                greet({"stream": h, "cross": 0})
+
+        for d in (1, n_cross - 1):
+            greet(device((0, d)))
+        pl.when(outer)(lambda: greet(device((1, 0))))
+        pl.when(inner)(lambda: greet(device((n_stream - 1, 0))))
+
+        @pl.when(early)
+        def _():
+            for p in others:
+                greet(device(p))
+
+        sides = jnp.where(inner, 1, 0) + jnp.where(outer, 1, 0)
+        expected = 2 + sides + jnp.where(early, HUBS - 1 + size - 1, HUBS)
+    else:
+        for p in across + along:
+            greet(device(p))
+        expected = n_cross + n_stream - 2
+
+    def remote(src, dst, send, recv, target):
+        return pltpu.make_async_remote_copy(
+            src_ref=src,
+            dst_ref=dst,
+            send_sem=send,
+            recv_sem=recv,
+            device_id=target,
+            device_id_type=MESH,
+        )
+
+    def spread(slot, buffer, offsets, send, recv):
+        return [
+            remote(mine.at[slot], buffer.at[i], send, recv, device(p))
+            for i, p in enumerate(offsets)
+        ]
+
+    def arrivals(buffer, count, recv):
+        part = buffer.at[pl.ds(0, count)]
+        pltpu.make_async_copy(part, part, recv).wait()
+
+    first_out, first_in = first_send.at[0], first_recv.at[0]
+    second_out, second_in = second_send.at[0], second_recv.at[0]
+    if direct:
+        spot_here = ms * n_cross + mc
+        to_hub = [
+            remote(
+                mine.at[0],
+                top_first.at[spot_here],
+                first_send.at[h],
+                first_in,
+                {"stream": h, "cross": 0},
+            )
+            for h in range(HUBS)
+        ]
+        cast = [
+            remote(mine.at[1], mine.at[2], second_out, second_in, {"stream": d, "cross": e})
+            for e in range(n_cross)
+            for d in range(n_stream)
+            if e > 0 or d >= HUBS
+        ]
+    else:
+        first = spread(0, top_first, across, first_out, first_in)
+        second = spread(1, top_second, along, second_out, second_in)
+
+    def greet_and_reduce():
+        pl.semaphore_wait(barrier, expected)
+        if direct:
+            for h in range(HUBS):
+                pl.when(jnp.logical_not(hubs[h]))(to_hub[h].start)
+        else:
+            for copy in first:
+                copy.start()
+
     loads[0].wait()
-
+    speed = None
+    for z in range(cz):
+        s = max_speed(primitive([base[v, z] for v in range(VARS)]))
+        speed = s if speed is None else jnp.maximum(speed, s)
+    mine[0] = jnp.max(speed, axis=0, keepdims=True)
+    if direct:
+        top_first[spot_here] = mine[0]
+
+    if direct:
+        pl.when(jnp.logical_not(early))(greet_and_reduce)
+    else:
+        greet_and_reduce()
+
+    loads[1].wait()
     lane = lax.broadcasted_iota(jnp.int32, (ny, nx), 1)
     group = lane // GROUP
     packed = [None] * VARS
@@ -210,14 +315,6 @@
             wy[pl.ds((HALO + y) * ztile + v * cz, cz), :] = wz[
                 pl.ds(HALO * tile + v * ny + y, cz, stride=tile), :
             ]
-    loads[1].wait()
-    speed = None
-    for z in range(cz):
-        s = max_speed(primitive([base[v, z] for v in range(VARS)]))
-        speed = s if speed is None else jnp.maximum(speed, s)
-    mine[0] = jnp.max(speed, axis=0, keepdims=True)
-
-    pl.semaphore_wait(barrier, n_cross - 1 + n_stream - 1)
 
     rows = HALO * ztile
     halo_y = [
@@ -226,7 +323,7 @@
             dst_ref=wy.at[pl.ds((HALO + ny) * ztile, rows)],
             send_sem=halo_send.at[0],
             recv_sem=halo_recv.at[0],
-            device_id={"cross": lax.rem(mc + n_cross - 1, n_cross)},
+            device_id=device((0, n_cross - 1)),
             device_id_type=MESH,
         ),
         pltpu.make_async_remote_copy(
@@ -234,7 +331,7 @@
             dst_ref=wy.at[pl.ds(0, rows)],
             send_sem=halo_send.at[1],
             recv_sem=halo_recv.at[1],
-            device_id={"cross": lax.rem(mc + 1, n_cross)},
+            device_id=device((0, 1)),
             device_id_type=MESH,
         ),
     ]
@@ -243,7 +340,7 @@
         dst_ref=from_low,
         send_sem=halo_send.at[2],
         recv_sem=halo_recv.at[2],
-        device_id={"stream": lax.rem(ms + 1, n_stream)},
+        device_id=device((1, 0)),
         device_id_type=MESH,
     )
     to_low = pltpu.make_async_remote_copy(
@@ -251,40 +348,22 @@
         dst_ref=from_high,
         send_sem=halo_send.at[3],
         recv_sem=halo_recv.at[3],
-        device_id={"stream": lax.rem(ms + n_stream - 1, n_stream)},
+        device_id=device((n_stream - 1, 0)),
         device_id_type=MESH,
     )
 
-    def reduce_copies(slot, buffer, axis, size, me, send, recv):
-        return [
-            pltpu.make_async_remote_copy(
-                src_ref=mine.at[slot],
-                dst_ref=buffer.at[d - 1],
-                send_sem=send.at[d - 1],
-                recv_sem=recv.at[d - 1],
-                device_id={axis: lax.rem(me + d, size)},
-                device_id_type=MESH,
-            )
-            for d in range(1, size)
-        ]
-
-    over_cross = reduce_copies(0, top_cross, "cross", n_cross, mc, cross_send, cross_recv)
-    over_stream = reduce_copies(1, top_stream, "stream", n_stream, ms, stream_send, stream_recv)
-
-    for copy in over_cross:
-        copy.start()
-
-    @pl.when(ms < n_stream - 1)
-    def _():
-        to_high.start()
-
-    @pl.when(ms > 0)
-    def _():
-        to_low.start()
-
-    for copy in halo_y:
-        copy.start()
-    loads[2].wait()
+    def send_up():
+        halo_y[1].start()
+        pl.when(outer)(to_high.start)
+        pl.when(inner)(to_low.start)
+
+    def send_down():
+        halo_y[0].start()
+
+    if direct:
+        pl.when(jnp.logical_not(early))(send_up)
+    else:
+        send_up()
 
     def stream_shifts(w):
         return [[pltpu.roll(x, d % nx, 1) for x in w] for d in (2, 1, -1, -2)]
@@ -304,7 +383,12 @@
         for v in range(VARS):
             total[cell_rows(v, z), :] = out[v]
 
-    sweep(wz, 0, cz, ny, 2, keep_rate)
+    sweep(wz, cz, ny, 2, keep_rate)
+
+    if direct:
+        pl.when(jnp.logical_not(early))(send_down)
+    else:
+        send_down()
 
     whole = (lane >= HALO) & (lane < nx - 2)
 
@@ -356,12 +440,80 @@
         for k in reversed(range(z - cz + 1, depth)):
             stages[k](z - k)
 
-    for copy in over_cross:
-        copy.wait_recv()
-    slab = mine[0]
-    for d in range(1, n_cross):
-        slab = jnp.maximum(slab, top_cross[d - 1])
-    mine[1] = slab
+    def add_rate(y, out):
+        for v in range(VARS):
+            rows = pl.ds(v * cz * ny + y, cz, stride=ny)
+            total[rows, :] = total[rows, :] + out[v]
+
+    wy_at, wy_row, wy_states = reader(wy, cz)
+
+    def cross_face(y, left, right):
+        return faces(left, right, wy_row(HALO + y - 1), wy_row(HALO + y), 1)
+
+    def cross_rate(y, lo, hi):
+        add_rate(y, rate(lo, hi, wy_at(HALO + y, 6)))
+
+    def save(slot, values):
+        for k, x in enumerate(values):
+            joint[slot, k] = x
+
+    def saved(slot, size):
+        return [joint[slot, k] for k in range(size)]
+
+    left, right = wy_states(2 * HALO - 1)
+    save(0, right)
+    lo = None
+    for y in range(HALO, ny - HALO + 1):
+        after, right = wy_states(HALO + y)
+        hi = cross_face(y, left, right)
+        if lo is None:
+            save(1, hi)
+        else:
+            cross_rate(y - 1, lo, hi)
+        left, lo = after, hi
+    save(2, left)
+    save(3, lo)
+
+    def low_edge():
+        left, _ = wy_states(HALO - 1)
+        lo = None
+        for y in range(HALO):
+            if y < HALO - 1:
+                after, right = wy_states(HALO + y)
+            else:
+                after, right = None, saved(0, VARS)
+            hi = cross_face(y, left, right)
+            if lo is not None:
+                cross_rate(y - 1, lo, hi)
+            left, lo = after, hi
+        cross_rate(HALO - 1, lo, saved(1, VARS + 1))
+
+    def high_edge():
+        left, lo = saved(2, VARS), saved(3, VARS + 1)
+        for y in range(ny - HALO + 1, ny + 1):
+            after, right = wy_states(HALO + y)
+            hi = cross_face(y, left, right)
+            cross_rate(y - 1, lo, hi)
+            left, lo = after, hi
+
+    if direct:
+
+        @pl.when(early)
+        def _():
+            greet_and_reduce()
+            send_up()
+            send_down()
+
+    else:
+        arrivals(top_first, len(across), first_in)
+        slab = mine[0]
+        for d in range(len(across)):
+            slab = jnp.maximum(slab, top_first[d])
+        mine[1] = slab
+        for copy in second:
+            copy.start()
+
+    loads[2].wait()
 
     @pl.when(ms == 0)
     def _():
@@ -373,9 +525,6 @@
         w = primitive([turned[v * ny : (v + 1) * ny] for v in range(VARS)])
         for v in range(VARS):
             from_low[pl.ds(v * ny, ny), :] = w[v]
-
-    for copy in over_stream:
-        copy.start()
 
     @pl.when(ms > 0)
     def _():
@@ -427,35 +576,55 @@
             total[rows, :] = total[rows, :] + jnp.where(rim, patch, 0.0)
             kept[rows, :] = base[v, z] * (1.0 / 3.0) + (2.0 / 3.0) * now[v, z]
 
-    def add_rate(y, out):
-        for v in range(VARS):
-            rows = pl.ds(v * cz * ny + y, cz, stride=ny)
-            total[rows, :] = total[rows, :] + out[v]
-
-    sweep(wy, HALO, ny - 2 * HALO, cz, 1, add_rate)
     halo_y[0].wait_recv()
-    sweep(wy, ny - HALO, HALO, cz, 1, add_rate)
+    high_edge()
+
+    if direct:
+
+        @pl.when(early)
+        def _():
+            arrivals(top_first, size - 1, first_in)
+            top = top_first[0]
+            for d in range(1, size):
+                top = jnp.maximum(top, top_first[d])
+            mine[1] = top
+            mine[2] = top
+
+        @pl.when(caster)
+        def _():
+            for copy in cast:
+                copy.start()
+
     halo_y[1].wait_recv()
-    sweep(wy, 0, HALO, cz, 1, add_rate)
-
-    for copy in over_stream:
-        copy.wait_recv()
-    top = mine[1]
-    for d in range(1, n_stream):
-        top = jnp.maximum(top, top_stream[d - 1])
+    low_edge()
+
+    for copy in halo_y:
+        copy.wait_send()
+    pl.when(outer)(to_high.wait_send)
+    pl.when(inner)(to_low.wait_send)
+
+    if direct:
+        for h in range(HUBS):
+            pl.when(jnp.logical_not(hubs[h]))(to_hub[h].wait_send)
+
+        @pl.when(caster)
+        def _():
+            arrivals(top_first, len(cast), second_out)
+
+        @pl.when(jnp.logical_not(early))
+        def _():
+            cast[0].wait_recv()
+
+        top = mine[2]
+    else:
+        arrivals(top_first, len(across), first_out)
+        arrivals(top_second, len(along), second_out)
+        arrivals(top_second, len(along), second_in)
+        top = mine[1]
+        for d in range(len(along)):
+            top = jnp.maximum(top, top_second[d])
     step = (2.0 / 3.0 * 0.3) / jnp.max(top, keepdims=True)
     scale[...] = jnp.broadcast_to(step, (ny, nx))
-
-    for copy in halo_y + over_cross + over_stream:
-        copy.wait_send()
-
-    @pl.when(ms < n_stream - 1)
-    def _():
-        to_high.wait_send()
-
-    @pl.when(ms > 0)
-    def _():
-        to_low.wait_send()
 
 
 def finish(ny, kept, total, scale, out_ref):
@@ -467,6 +636,8 @@
 
 def solution(mesh):
     n_stream, n_cross = mesh.shape["stream"], mesh.shape["cross"]
+    direct = n_stream * n_cross <= DIRECT
+    first = n_stream * n_cross if direct else n_cross - 1
 
     def shards(state_now, state_base, inflow):
         _, cz, ny, nx = state_now.shape
@@ -475,7 +646,7 @@
         dma = lambda n: pltpu.SemaphoreType.DMA((n,))
         cells = VARS * cz * ny
         kept, total, scale = pl.pallas_call(
-            functools.partial(kernel, (n_stream, n_cross, cz, ny, nx)),
+            functools.partial(kernel, (n_stream, n_cross, cz, ny, nx), direct),
             out_shape=(
                 vmem(cells, nx),
                 vmem(cells, nx),
@@ -497,16 +668,17 @@
                 vmem(VARS * ny, nx),
                 vmem(VARS * ny, nx),
                 vmem(VARS * ny, nx),
-                vmem(n_cross - 1, 1, nx),
+                vmem(4, VARS + 1, cz, nx),
+                vmem(first, 1, nx),
                 vmem(n_stream - 1, 1, nx),
-                vmem(2, 1, nx),
+                vmem(3, 1, nx),
                 dma(3),
                 dma(4),
                 dma(4),
-                dma(n_cross - 1),
-                dma(n_cross - 1),
-                dma(n_stream - 1),
-                dma(n_stream - 1),
+                dma(HUBS),
+                dma(1),
+                dma(1),
+                dma(1),
             ],
             compiler_params=pltpu.CompilerParams(collective_id=0, has_side_effects=True),
         )(state_now, state_base, jnp.transpose(inflow, (0, 3, 1, 2)))

time: 13.2 us -> 12 us (0.909)
  the two profiles are of different devices: /device:TPU:0 before, /device:TPU:1 now
where the time goes in v1:
time: 12 us; the launch traced here: 11.9 us
  Pallas kernels  11.9 us (99%)
    pallas_call x1, Pallas kernels, shards(): pl.pallas_call(functools.partial(kernel, (n_stream, n_cross, cz, ny, nx),...  11.2 us
    pallas_call x1, Pallas kernels, shards(): pl.pallas_call(functools.partial(finish, ny), out_shape=jax.ShapeDtypeStr...  0.71 us

profile of v1, /device:TPU:1, one launch (start us, length us, event | category | flops | bytes accessed | tf_op | source)
XLA Modules:
  0.0 11.9 jit_solution(9499331203504541536)
XLA Ops:
  0.0 11.2 %shard_map.37 = (f32[448,128]{1,0:T(8,128)S(1)}, f32[448,128]{1,0:T(8,128)S(1)}, f32[8,128]{1,0:T(8,128)S(1)}) custom-call(f32[7,8,8,128]{3,2,1,0:T(8,128)} %now_hbm.1, f32[7,8,8,128]{3,2,1,0:T(8,128)} %base_hbm.1, f32[7,3,8,8]{3,2,1,0:T(8,128)} %bitcast.2), custom_call_target="tpu_custom_call" | custom-call | tf_op jit(solution)/shard_map/pallas_call | solution.py:648
  11.2 0.7 %shard_map.38 = f32[448,128]{1,0:T(8,128)} custom-call(f32[448,128]{1,0:T(8,128)S(1)} %get-tuple-element.8.kept, f32[448,128]{1,0:T(8,128)S(1)} %get-tuple-element.9.total, f32[8,128]{1,0:T(8,128)S(1)} %get-tuple-element.10.scale), custom_call_target="tpu_custom_call" | custom-call | tf_op jit(solution)/shard_map/pallas_call | solution.py:688

commit v2 on v1

--- a/solution.py
+++ b/solution.py
@@ -161,6 +161,7 @@
     first_recv,
     second_send,
     second_recv,
+    ready_sem,
 ):
     n_stream, n_cross, cz, ny, nx = dims
     tile = VARS * ny
@@ -181,7 +182,8 @@
     along = [(d, 0) for d in range(1, n_stream)]
     others = [(d, e) for e in range(n_cross) for d in range(n_stream) if (d, e) != (0, 0)]
     inner, outer = ms > 0, ms < n_stream - 1
-    hubs = [(ms == h) & (mc == 0) for h in range(HUBS)]
+    lowest, highest = mc == 0, mc == n_cross - 1
+    hubs = [(ms == h) & lowest for h in range(HUBS)]
     early = functools.reduce(jnp.logical_or, hubs)
     caster = hubs[HUBS - 1]
 
@@ -196,29 +198,37 @@
     def greet(target):
         pl.semaphore_signal(barrier, device_id=target, device_id_type=MESH)
 
-    if direct:
-        for h in range(HUBS):
-
-            @pl.when(jnp.logical_not(hubs[h]))
-            def _(h=h):
-                greet({"stream": h, "cross": 0})
-
-        for d in (1, n_cross - 1):
-            greet(device((0, d)))
-        pl.when(outer)(lambda: greet(device((1, 0))))
-        pl.when(inner)(lambda: greet(device((n_stream - 1, 0))))
+    above, below = device((0, 1)), device((0, n_cross - 1))
+    after, before = device((1, 0)), device((n_stream - 1, 0))
+
+    def ready(k, target):
+        pl.semaphore_signal(ready_sem.at[k], device_id=target, device_id_type=MESH)
+
+    def await_ready(k):
+        pl.semaphore_wait(ready_sem.at[k], 1)
+
+    if direct:
+        pl.when(jnp.logical_not(highest))(lambda: greet(above))
+        pl.when(lowest)(lambda: greet(below))
+        pl.when(outer)(lambda: greet(after))
 
         @pl.when(early)
         def _():
             for p in others:
                 greet(device(p))
 
-        sides = jnp.where(inner, 1, 0) + jnp.where(outer, 1, 0)
-        expected = 2 + sides + jnp.where(early, HUBS - 1 + size - 1, HUBS)
+        one = lambda flag: jnp.where(flag, 1, 0)
+        greetings = jnp.where(early, HUBS - 1, HUBS)
+        pl.semaphore_wait(
+            barrier, greetings + one(inner) + one(highest) + one(jnp.logical_not(lowest))
+        )
+        pl.when(highest)(lambda: ready(2, above))
+        pl.when(jnp.logical_not(lowest))(lambda: ready(0, below))
+        pl.when(inner)(lambda: ready(1, before))
     else:
         for p in across + along:
             greet(device(p))
-        expected = n_cross + n_stream - 2
+        pl.semaphore_wait(barrier, n_cross + n_stream - 2)
 
     def remote(src, dst, send, recv, target):
         return pltpu.make_async_remote_copy(
@@ -264,57 +274,13 @@
         first = spread(0, top_first, across, first_out, first_in)
         second = spread(1, top_second, along, second_out, second_in)
 
-    def greet_and_reduce():
-        pl.semaphore_wait(barrier, expected)
+    def send_speed():
         if direct:
             for h in range(HUBS):
                 pl.when(jnp.logical_not(hubs[h]))(to_hub[h].start)
         else:
             for copy in first:
                 copy.start()
-
-    loads[0].wait()
-    speed = None
-    for z in range(cz):
-        s = max_speed(primitive([base[v, z] for v in range(VARS)]))
-        speed = s if speed is None else jnp.maximum(speed, s)
-    mine[0] = jnp.max(speed, axis=0, keepdims=True)
-    if direct:
-        top_first[spot_here] = mine[0]
-
-    if direct:
-        pl.when(jnp.logical_not(early))(greet_and_reduce)
-    else:
-        greet_and_reduce()
-
-    loads[1].wait()
-    lane = lax.broadcasted_iota(jnp.int32, (ny, nx), 1)
-    group = lane // GROUP
-    packed = [None] * VARS
-    for z in range(cz):
-        w = primitive([now[v, z] for v in range(VARS)])
-        spots = [HALO + z]
-        if z < HALO:
-            spots.append(HALO + cz + z)
-        if z >= cz - HALO:
-            spots.append(z - (cz - HALO))
-        for v in range(VARS):
-            for c in spots:
-                wz[pl.ds(c * tile + v * ny, ny), :] = w[v]
-            upper = pltpu.roll(w[v], (GROUP * z - (nx - 5)) % nx, 1)
-            lower = pltpu.roll(w[v], (half + GROUP * z + HALO) % nx, 1)
-            piece = jnp.where(group == z, upper, lower)
-            if z == 0:
-                packed[v] = piece
-            else:
-                packed[v] = jnp.where((group == z) | (group == cz + z), piece, packed[v])
-    for v in range(VARS):
-        pack[pl.ds(v * ny, ny), :] = packed[v]
-    for y in range(ny):
-        for v in range(VARS):
-            wy[pl.ds((HALO + y) * ztile + v * cz, cz), :] = wz[
-                pl.ds(HALO * tile + v * ny + y, cz, stride=tile), :
-            ]
 
     rows = HALO * ztile
     halo_y = [
@@ -323,7 +289,7 @@
             dst_ref=wy.at[pl.ds((HALO + ny) * ztile, rows)],
             send_sem=halo_send.at[0],
             recv_sem=halo_recv.at[0],
-            device_id=device((0, n_cross - 1)),
+            device_id=below,
             device_id_type=MESH,
         ),
         pltpu.make_async_remote_copy(
@@ -331,7 +297,7 @@
             dst_ref=wy.at[pl.ds(0, rows)],
             send_sem=halo_send.at[1],
             recv_sem=halo_recv.at[1],
-            device_id=device((0, 1)),
+            device_id=above,
             device_id_type=MESH,
         ),
     ]
@@ -340,7 +306,7 @@
         dst_ref=from_low,
         send_sem=halo_send.at[2],
         recv_sem=halo_recv.at[2],
-        device_id=device((1, 0)),
+        device_id=after,
         device_id_type=MESH,
     )
     to_low = pltpu.make_async_remote_copy(
@@ -348,22 +314,80 @@
         dst_ref=from_high,
         send_sem=halo_send.at[3],
         recv_sem=halo_recv.at[3],
-        device_id=device((n_stream - 1, 0)),
+        device_id=before,
         device_id_type=MESH,
     )
 
     def send_up():
         halo_y[1].start()
-        pl.when(outer)(to_high.start)
-        pl.when(inner)(to_low.start)
+
+    def send_up_ready():
+        await_ready(0)
+        halo_y[1].start()
 
     def send_down():
         halo_y[0].start()
 
-    if direct:
-        pl.when(jnp.logical_not(early))(send_up)
+    def send_down_around():
+        await_ready(2)
+        halo_y[0].start()
+
+    def send_after():
+        if direct:
+            await_ready(1)
+        to_high.start()
+
+    def by_plane(y):
+        for v in range(VARS):
+            wy[pl.ds((HALO + y) * ztile + v * cz, cz), :] = wz[
+                pl.ds(HALO * tile + v * ny + y, cz, stride=tile), :
+            ]
+
+    loads[0].wait()
+    speed = None
+    for z in range(cz):
+        s = max_speed(primitive([base[v, z] for v in range(VARS)]))
+        speed = s if speed is None else jnp.maximum(speed, s)
+    mine[0] = jnp.max(speed, axis=0, keepdims=True)
+    if direct:
+        top_first[spot_here] = mine[0]
+    send_speed()
+
+    loads[1].wait()
+    lane = lax.broadcasted_iota(jnp.int32, (ny, nx), 1)
+    group = lane // GROUP
+    for z in range(cz):
+        w = primitive([now[v, z] for v in range(VARS)])
+        spots = [HALO + z]
+        if z < HALO:
+            spots.append(HALO + cz + z)
+        if z >= cz - HALO:
+            spots.append(z - (cz - HALO))
+        for v in range(VARS):
+            for c in spots:
+                wz[pl.ds(c * tile + v * ny, ny), :] = w[v]
+    for y in range(ny):
+        by_plane(y)
+    if direct:
+        pl.when(highest)(send_up)
+        pl.when(jnp.logical_not(highest | lowest))(send_down)
     else:
         send_up()
+        send_down()
+
+    for v in range(VARS):
+        packed = None
+        for z in range(cz):
+            w = wz[pl.ds((HALO + z) * tile + v * ny, ny), :]
+            upper = pltpu.roll(w, (GROUP * z - (nx - 5)) % nx, 1)
+            lower = pltpu.roll(w, (half + GROUP * z + HALO) % nx, 1)
+            piece = jnp.where(group == z, upper, lower)
+            if z == 0:
+                packed = piece
+            else:
+                packed = jnp.where((group == z) | (group == cz + z), piece, packed)
+        pack[pl.ds(v * ny, ny), :] = packed
+    pl.when(inner)(to_low.start)
 
     def stream_shifts(w):
         return [[pltpu.roll(x, d % nx, 1) for x in w] for d in (2, 1, -1, -2)]
@@ -385,10 +409,9 @@
 
     sweep(wz, cz, ny, 2, keep_rate)
 
-    if direct:
-        pl.when(jnp.logical_not(early))(send_down)
-    else:
-        send_down()
+    pl.when(outer)(send_after)
+    if direct:
+        pl.when(jnp.logical_not(highest))(send_up_ready)
 
     whole = (lane >= HALO) & (lane < nx - 2)
 
@@ -439,6 +462,9 @@
     for z in range(cz, cz + depth - 1):
         for k in reversed(range(z - cz + 1, depth)):
             stages[k](z - k)
+
+    if direct:
+        pl.when(highest)(send_down)
 
     def add_rate(y, out):
         for v in range(VARS):
@@ -496,15 +522,7 @@
             cross_rate(y - 1, lo, hi)
             left, lo = after, hi
 
-    if direct:
-
-        @pl.when(early)
-        def _():
-            greet_and_reduce()
-            send_up()
-            send_down()
-
-    else:
+    if not direct:
         arrivals(top_first, len(across), first_in)
         slab = mine[0]
         for d in range(len(across)):
@@ -576,6 +594,8 @@
             total[rows, :] = total[rows, :] + jnp.where(rim, patch, 0.0)
             kept[rows, :] = base[v, z] * (1.0 / 3.0) + (2.0 / 3.0) * now[v, z]
 
+    if direct:
+        pl.when(lowest)(send_down_around)
     halo_y[0].wait_recv()
     high_edge()
 
@@ -679,6 +699,7 @@
                 dma(1),
                 dma(1),
                 dma(1),
+                pltpu.SemaphoreType.REGULAR((3,)),
             ],
             compiler_params=pltpu.CompilerParams(collective_id=0, has_side_effects=True),
         )(state_now, state_base, jnp.transpose(inflow, (0, 3, 1, 2)))

time: 12 us -> 11.1 us (0.925)
  the two profiles are of different devices: /device:TPU:1 before, /device:TPU:0 now
where the time goes in v2:
time: 11.1 us; the launch traced here: 11 us
  Pallas kernels  11 us (99%)
    pallas_call x1, Pallas kernels, shards(): pl.pallas_call(functools.partial(kernel, (n_stream, n_cross, cz, ny, nx),...  10.2 us
    pallas_call x1, Pallas kernels, shards(): pl.pallas_call(functools.partial(finish, ny), out_shape=jax.ShapeDtypeStr...  0.71 us

profile of v2, /device:TPU:0, one launch (start us, length us, event | category | flops | bytes accessed | tf_op | source)
XLA Modules:
  0.0 11.0 jit_solution(3138554530276199650)
XLA Ops:
  0.0 10.2 %shard_map.37 = (f32[448,128]{1,0:T(8,128)S(1)}, f32[448,128]{1,0:T(8,128)S(1)}, f32[8,128]{1,0:T(8,128)S(1)}) custom-call(f32[7,8,8,128]{3,2,1,0:T(8,128)} %now_hbm.1, f32[7,8,8,128]{3,2,1,0:T(8,128)} %base_hbm.1, f32[7,3,8,8]{3,2,1,0:T(8,128)} %bitcast.2), custom_call_target="tpu_custom_call" | custom-call | tf_op jit(solution)/shard_map/pallas_call | solution.py:668
  10.3 0.7 %shard_map.38 = f32[448,128]{1,0:T(8,128)} custom-call(f32[448,128]{1,0:T(8,128)S(1)} %get-tuple-element.8.kept, f32[448,128]{1,0:T(8,128)S(1)} %get-tuple-element.9.total, f32[8,128]{1,0:T(8,128)S(1)} %get-tuple-element.10.scale), custom_call_target="tpu_custom_call" | custom-call | tf_op jit(solution)/shard_map/pallas_call | solution.py:709

commit v3 on v2

--- a/solution.py
+++ b/solution.py
@@ -174,8 +174,11 @@
         pltpu.make_async_copy(now_hbm, now, load_sem.at[1]),
         pltpu.make_async_copy(inflow_hbm, inflow, load_sem.at[2]),
     ]
-    for copy in loads:
-        copy.start()
+    for v in range(VARS):
+        pltpu.make_async_copy(base_hbm.at[v], base.at[v], load_sem.at[0]).start()
+    for v in range(VARS):
+        pltpu.make_async_copy(now_hbm.at[v], now.at[v], load_sem.at[1]).start()
+    loads[2].start()
 
     size = n_stream * n_cross
     across = [(0, d) for d in range(1, n_cross)]
@@ -283,54 +286,54 @@
                 copy.start()
 
     rows = HALO * ztile
-    halo_y = [
-        pltpu.make_async_remote_copy(
-            src_ref=wy.at[pl.ds(rows, rows)],
-            dst_ref=wy.at[pl.ds((HALO + ny) * ztile, rows)],
-            send_sem=halo_send.at[0],
-            recv_sem=halo_recv.at[0],
-            device_id=below,
-            device_id_type=MESH,
-        ),
-        pltpu.make_async_remote_copy(
-            src_ref=wy.at[pl.ds(ny * ztile, rows)],
-            dst_ref=wy.at[pl.ds(0, rows)],
-            send_sem=halo_send.at[1],
-            recv_sem=halo_recv.at[1],
-            device_id=above,
-            device_id_type=MESH,
-        ),
+    down = remote(
+        wy.at[pl.ds(rows, rows)],
+        wy.at[pl.ds((HALO + ny) * ztile, rows)],
+        halo_send.at[0],
+        halo_recv.at[0],
+        below,
+    )
+    up = [
+        remote(
+            wy.at[pl.ds((ny + k) * ztile, ztile)],
+            wy.at[pl.ds(k * ztile, ztile)],
+            halo_send.at[3 + k],
+            halo_recv.at[3 + k],
+            above,
+        )
+        for k in range(HALO)
     ]
     to_high = pltpu.make_async_remote_copy(
         src_ref=pack,
         dst_ref=from_low,
-        send_sem=halo_send.at[2],
-        recv_sem=halo_recv.at[2],
+        send_sem=halo_send.at[1],
+        recv_sem=halo_recv.at[1],
         device_id=after,
         device_id_type=MESH,
     )
     to_low = pltpu.make_async_remote_copy(
         src_ref=pack,
         dst_ref=from_high,
-        send_sem=halo_send.at[3],
-        recv_sem=halo_recv.at[3],
+        send_sem=halo_send.at[2],
+        recv_sem=halo_recv.at[2],
         device_id=before,
         device_id_type=MESH,
     )
 
     def send_up():
-        halo_y[1].start()
+        for copy in reversed(up):
+            copy.start()
 
     def send_up_ready():
         await_ready(0)
-        halo_y[1].start()
+        send_up()
 
     def send_down():
-        halo_y[0].start()
+        down.start()
 
     def send_down_around():
         await_ready(2)
-        halo_y[0].start()
+        down.start()
 
     def send_after():
         if direct:
@@ -500,19 +503,17 @@
     save(2, left)
     save(3, lo)
 
-    def low_edge():
-        left, _ = wy_states(HALO - 1)
-        lo = None
-        for y in range(HALO):
-            if y < HALO - 1:
-                after, right = wy_states(HALO + y)
-            else:
-                after, right = None, saved(0, VARS)
-            hi = cross_face(y, left, right)
-            if lo is not None:
-                cross_rate(y - 1, lo, hi)
-            left, lo = after, hi
-        cross_rate(HALO - 1, lo, saved(1, VARS + 1))
+    def low_edge(cells, joint_in, joint_out):
+        ahead_flux, next_right = saved(joint_in[1], VARS + 1), saved(joint_in[0], VARS)
+        for y in cells:
+            up[y].wait_recv()
+            left, right = wy_states(HALO + y - 1)
+            lo = cross_face(y, left, next_right)
+            cross_rate(y, lo, ahead_flux)
+            ahead_flux, next_right = lo, right
+        if joint_out:
+            save(joint_out[0], next_right)
+            save(joint_out[1], ahead_flux)
 
     def high_edge():
         left, lo = saved(2, VARS), saved(3, VARS + 1)
@@ -596,8 +597,14 @@
 
     if direct:
         pl.when(lowest)(send_down_around)
-    halo_y[0].wait_recv()
+    down.wait_recv()
     high_edge()
+
+    def set_scale(top):
+        step = (2.0 / 3.0 * 0.3) / jnp.max(top, keepdims=True)
+        scale[...] = jnp.broadcast_to(step, (ny, nx))
+
+    low_edge(range(HALO - 1, 0, -1), (0, 1), (4, 5))
 
     if direct:
 
@@ -608,24 +615,29 @@
             for d in range(1, size):
                 top = jnp.maximum(top, top_first[d])
             mine[1] = top
-            mine[2] = top
-
-        @pl.when(caster)
-        def _():
-            for copy in cast:
-                copy.start()
-
-    halo_y[1].wait_recv()
-    low_edge()
-
-    for copy in halo_y:
+
+            @pl.when(caster)
+            def _():
+                for copy in cast:
+                    copy.start()
+
+            set_scale(top)
+
+    down.wait_send()
+    for copy in up:
         copy.wait_send()
     pl.when(outer)(to_high.wait_send)
     pl.when(inner)(to_low.wait_send)
-
     if direct:
         for h in range(HUBS):
             pl.when(jnp.logical_not(hubs[h]))(to_hub[h].wait_send)
+    else:
+        arrivals(top_first, len(across), first_out)
+        arrivals(top_second, len(along), second_out)
+
+    low_edge([0], (4, 5), None)
+
+    if direct:
 
         @pl.when(caster)
         def _():
@@ -634,17 +646,14 @@
         @pl.when(jnp.logical_not(early))
         def _():
             cast[0].wait_recv()
-
-        top = mine[2]
+            set_scale(mine[2])
+
     else:
-        arrivals(top_first, len(across), first_out)
-        arrivals(top_second, len(along), second_out)
         arrivals(top_second, len(along), second_in)
         top = mine[1]
         for d in range(len(along)):
             top = jnp.maximum(top, top_second[d])
-    step = (2.0 / 3.0 * 0.3) / jnp.max(top, keepdims=True)
-    scale[...] = jnp.broadcast_to(step, (ny, nx))
+        set_scale(top)
 
 
 def finish(ny, kept, total, scale, out_ref):
@@ -688,13 +697,13 @@
                 vmem(VARS * ny, nx),
                 vmem(VARS * ny, nx),
                 vmem(VARS * ny, nx),
-                vmem(4, VARS + 1, cz, nx),
+                vmem(6, VARS + 1, cz, nx),
                 vmem(first, 1, nx),
                 vmem(n_stream - 1, 1, nx),
                 vmem(3, 1, nx),
                 dma(3),
-                dma(4),
-                dma(4),
+                dma(3 + HALO),
+                dma(3 + HALO),
                 dma(HUBS),
                 dma(1),
                 dma(1),

time: 11.1 us -> 10.8 us (0.973)
  Pallas kernels: 11 us -> 10.6 us
    pallas_call x1, Pallas kernels: 10.2 us -> 9.91 us  [shards(): pl.pallas_call(functools.partial(kernel, (n_stream, n_cross, cz, ny, nx),...]
where the time goes in v3:
time: 10.8 us; the launch traced here: 10.6 us
  Pallas kernels  10.6 us (98%)
    pallas_call x1, Pallas kernels, shards(): pl.pallas_call(functools.partial(kernel, (n_stream, n_cross, cz, ny, nx),...  9.91 us
    pallas_call x1, Pallas kernels, shards(): pl.pallas_call(functools.partial(finish, ny), out_shape=jax.ShapeDtypeStr...  0.71 us

profile of v3, /device:TPU:0, one launch (start us, length us, event | category | flops | bytes accessed | tf_op | source)
XLA Modules:
  0.0 10.6 jit_solution(1240731597430700551)
XLA Ops:
  0.0 9.9 %shard_map.37 = (f32[448,128]{1,0:T(8,128)S(1)}, f32[448,128]{1,0:T(8,128)S(1)}, f32[8,128]{1,0:T(8,128)S(1)}) custom-call(f32[7,8,8,128]{3,2,1,0:T(8,128)} %now_hbm.1, f32[7,8,8,128]{3,2,1,0:T(8,128)} %base_hbm.1, f32[7,3,8,8]{3,2,1,0:T(8,128)} %bitcast.2), custom_call_target="tpu_custom_call" | custom-call | tf_op jit(solution)/shard_map/pallas_call | solution.py:677
  9.9 0.7 %shard_map.38 = f32[448,128]{1,0:T(8,128)} custom-call(f32[448,128]{1,0:T(8,128)S(1)} %get-tuple-element.8.kept, f32[448,128]{1,0:T(8,128)S(1)} %get-tuple-element.9.total, f32[8,128]{1,0:T(8,128)S(1)} %get-tuple-element.10.scale), custom_call_target="tpu_custom_call" | custom-call | tf_op jit(solution)/shard_map/pallas_call | solution.py:718
